TPU v7x, 16 devices: a 4x2x1 block of a 4x4x8 slice. The times are simulated.
16 devices in a mesh: dp: 2 (over y, z), dcp: 8 (over x, core).
Axes of the slice: x: 4, y: 2, z: 1, core: 2. Of those that a mesh axis runs over, the one named last changes fastest.
The devices are a block of a 4x4x8 slice.
Arguments:
- q_abs: bfloat16 [128, 2, 128, 576], P('dp', None, 'dcp'), parts along dimension 0
- kv_cache: bfloat16 [128, 16, 8, 64, 576], P('dp', None, 'dcp'), parts along dimension 0
- lengths: int32 [128], P('dp'), parts along dimension 0
Outputs:
- output: bfloat16 [128, 2, 128, 512], P('dp', None, 'dcp'), parts along dimension 0
There are 2 independent parts. A program takes and returns all parts, laid end to end along the dimension named above; each array names one.
All inputs are finite; a program needn't handle non-finite values.
Results may differ from a plain program's by a relative error of at most 0.00759048.
Values are sent between devices in bfloat16 or wider.
A program may use at most 768 MiB of HBM per device.

v0:
```python
import jax
import jax.numpy as jnp
from jax import lax
from jax.sharding import PartitionSpec as P

LATENT = 512
ROPE = 64
NOPE = 128
PAGE = 64
MASKED = -1e30


def solution(mesh):
    group_size = mesh.shape['dcp']
    score_scale = (NOPE + ROPE) ** -0.5

    def local_step(q_blk, kv_blk, len_blk):
        batch_loc, tok_count, heads_loc, q_width = q_blk.shape
        rounds = kv_blk.shape[1]
        local_keys = kv_blk.reshape(batch_loc, rounds * PAGE, q_width)
        q_all = lax.all_gather(q_blk, 'dcp', axis=2, tiled=True)
        scores = jnp.einsum('bthd,bsd->bths', q_all, local_keys, preferred_element_type=jnp.float32) * score_scale
        device = lax.axis_index('dcp')
        positions = ((jnp.arange(rounds)[:, None] * group_size + device) * PAGE + jnp.arange(PAGE)[None, :]).reshape(rounds * PAGE)
        last_pos = len_blk[:, None] - tok_count + jnp.arange(tok_count)[None, :]
        visible = positions[None, None, None, :] <= last_pos[:, :, None, None]
        scores = jnp.where(visible, scores, MASKED)
        row_max = jnp.max(scores, axis=-1)
        weights = jnp.exp(scores - row_max[..., None])
        row_sum = jnp.sum(weights, axis=-1)
        part_out = jnp.einsum('bths,bsc->bthc', weights.astype(jnp.bfloat16), local_keys[:, :, :LATENT], preferred_element_type=jnp.float32)
        part_out = (part_out / row_sum[..., None]).astype(jnp.bfloat16)
        part_lse = row_max + jnp.log(row_sum)
        recv_out = lax.all_to_all(part_out, 'dcp', 2, 2, tiled=True).reshape(batch_loc, tok_count, group_size, heads_loc, LATENT)
        recv_lse = lax.all_to_all(part_lse, 'dcp', 2, 2, tiled=True).reshape(batch_loc, tok_count, group_size, heads_loc)
        total_lse = jax.nn.logsumexp(recv_lse, axis=2, keepdims=True)
        merge_w = jnp.exp(recv_lse - total_lse)
        merged = jnp.sum(merge_w[..., None] * recv_out.astype(jnp.float32), axis=2)
        return merged.astype(jnp.bfloat16)

    return jax.shard_map(local_step, mesh=mesh, in_specs=(P('dp', None, 'dcp', None), P('dp', None, 'dcp', None, None), P('dp')), out_specs=P('dp', None, 'dcp', None), check_vma=False)
```

profile of v0, /device:TPU:112, one launch (start us, length us, event | category | flops | bytes accessed | tf_op | source)
XLA Modules:
  0.0 500.4 jit_solution(2862434368241799468)
XLA Ops:
  6.5 0.0 all-gather.2.cloned.1.call-start
  6.6 0.7 all-gather.2.cloned.1.call-update
  7.3 0.1 iota_add_fusion.1
  7.4 0.1 add.66
  7.5 0.7 broadcast_add_fusion
  8.1 0.1 iota_add_fusion
  8.2 0.4 broadcast_compare_fusion
  8.6 102.2 %all-gather.2.cloned.1.call-done = bf16[64,2,128,576]{3,2,1,0:T(8,128)(2,1)} async-done(((bf16[64,2,16,576]{3,2,1,0:T(8,128)(2,1)}), bf16[64,2,128,576]{3,2,1,0:T(8,128)(2,1)}) %all-gather.2.cloned.1.call-update) | async-done | bytes 18874384 | tf_op jit(solution)/shard_map/all_gather | solution.py:21
  110.7 65.5 %fusion.1 = (f32[64,2,128]{2,1,0:T(2,128)S(1)}, f32[64,2,128,1024]{3,2,1,0:T(8,128)}) fusion(pred[64,2,1024]{2,1,0:T(4,128)(4,1)S(1)} %broadcast_compare_fusion, bf16[64,2,128,576]{3,2,1,0:T(8,128)(2,1)} %all-gather.2.cloned.1.call-done, bf16[64,1024,576,1]{2,1,3,0:T(8,128)(2,1)} %bitcast.7), kind=kOutput, calls=%fused_computation.4 | convolution fusion | flops 19377668096 | bytes 161677312 | tf_op jit(solution)/shard_map/bthd,bsd->bths/dot_general | solution.py:22
  176.3 21.5 %fusion.3 = f32[64,2,128]{2,1,0:T(2,128)S(1)} fusion(f32[64,2,128,1024]{3,2,1,0:T(8,128)} %get-tuple-element.6, f32[64,2,128]{2,1,0:T(2,128)S(1)} %get-tuple-element.5, pred[64,2,1024]{2,1,0:T(4,128)(4,1)S(1)} %broadcast_compare_fusion), kind=kLoop, calls=%fused_computation.6 | loop fusion | flops 67092480 | bytes 67371008 | tf_op jit(solution)/shard_map/reduce_sum | solution.py:30
  197.8 0.1 copy.23
  197.9 0.8 reshape.89
  198.7 3.8 all-to-all-start
  202.5 48.7 %divide_convert_fusion = bf16[64,2,128,512]{3,2,1,0:T(8,128)(2,1)} fusion(f32[64,2,128]{2,1,0:T(2,128)S(1)} %fusion.3, bf16[64,1024,576]{2,1,0:T(8,128)(2,1)} %bitcast, f32[64,2,128,1024]{3,2,1,0:T(8,128)} %get-tuple-element.6, f32[64,2,128]{2,1,0:T(2,128)S(1)} %get-tuple-element.5, pred[64,2,1024]{2,1,0:T(4,128)(4,1)S(1)} %broadcast_compare_fusion), kind=kOutput, calls=%fused_computation.9 | convolution fusion | flops 17263755264 | bytes 151257088 | tf_op jit(solution)/shard_map/bths,bsc->bthc/dot_general | solution.py:31
  251.2 24.5 %copy.26 = bf16[64,2,128,512]{3,1,0,2:T(2,128)(2,1)} copy(bf16[64,2,128,512]{3,2,1,0:T(8,128)(2,1)} %divide_convert_fusion) | data formatting | bytes 33554432 | tf_op jit(solution)/shard_map/convert_element_type | solution.py:32
  275.7 0.0 all-to-all-done
  275.7 6.1 %all-to-all-start.1 = ((bf16[64,2,128,512]{3,1,0,2:T(2,128)(2,1)}), bf16[64,2,128,512]{3,1,0,2:T(2,128)(2,1)}, u32[]{:S(2)}, u32[]{:S(2)}) async-start(bf16[64,2,128,512]{3,1,0,2:T(2,128)(2,1)} %copy.26), calls=%async_computation.1 | async-start | bytes 33554432 | tf_op jit(solution)/shard_map/all_to_all | solution.py:34
  281.8 0.5 broadcast.75
  282.3 0.8 reduce
  283.2 0.1 reshape.90
  283.4 2.8 copy.25
  286.2 179.8 %all-to-all-done.1 = bf16[64,2,128,512]{3,1,0,2:T(2,128)(2,1)} async-done(((bf16[64,2,128,512]{3,1,0,2:T(2,128)(2,1)}), bf16[64,2,128,512]{3,1,0,2:T(2,128)(2,1)}, u32[]{:S(2)}, u32[]{:S(2)}) %all-to-all-start.1) | async-done | bytes 16777248 | tf_op jit(solution)/shard_map/all_to_all | solution.py:34
  466.0 24.0 %fusion.5 = bf16[64,2,16,512]{3,1,0,2:T(2,128)(2,1)S(1)} fusion(bf16[64,2,8,16,512]{4,1,0,3,2:T(2,128)(2,1)} %bitcast.9, f32[64,2,8,16]{1,0,3,2:T(8,128)} %copy.25), kind=kLoop, calls=%fused_computation.8 | loop fusion | flops 24117248 | bytes 18939904 | tf_op jit(solution)/shard_map/reduce_sum | solution.py:38
  490.0 3.5 copy.27
  (8 shorter events, 0.1 us)
Async XLA Ops:
  6.5 104.2 %all-gather.2.cloned.1.call-start = ((), (), s32[]{:S(2)}) async-start(), calls=%async_computation.2 | async-start | bytes 23592960 | tf_op jit(solution)/shard_map/all_gather | solution.py:21
  198.7 77.0 %all-to-all-start = ((f32[8,1,2048]{2,1,0:T(1,128)}), f32[8,1,2048]{2,1,0:T(1,128)S(1)}, u32[]{:S(2)}, u32[]{:S(2)}) async-start(f32[8,1,2048]{2,1,0:T(1,128)} %reshape.89), calls=%async_computation | async-start | bytes 131072 | tf_op jit(solution)/shard_map/all_to_all | solution.py:35
  275.7 190.3 %all-to-all-start.1 = ((bf16[64,2,128,512]{3,1,0,2:T(2,128)(2,1)}), bf16[64,2,128,512]{3,1,0,2:T(2,128)(2,1)}, u32[]{:S(2)}, u32[]{:S(2)}) async-start(bf16[64,2,128,512]{3,1,0,2:T(2,128)(2,1)} %copy.26), calls=%async_computation.1 | async-start | bytes 33554432 | tf_op jit(solution)/shard_map/all_to_all | solution.py:34
Sparse Core Ops, SparseCore 0:
  8.9 101.7 all-gather.1
where the time goes:
time: 501 us; the launch traced here: 500 us
  waiting for transfers between devices  283 us (56%)
  matrix products  114 us (23%)
  other arithmetic  47.6 us (10%)
  local copies, waits for them, and re-layouts  32.4 us (6%)
  between operations  13.5 us (3%)
  starting transfers between devices  9.89 us (2%)
    all_to_all x1, waiting for transfers between devices, local_step(): lax.all_to_all(part_out, 'dcp', 2, 2, tiled=True)  180 us
    all_gather x1, waiting for transfers between devices, local_step(): q_all = lax.all_gather(q_blk, 'dcp', axis=2, tiled=True)  102 us
    dot_general x1, matrix products, local_step(): jnp.einsum('bthd,bsd->bths', q_all, local_keys, preferred_element_type=jn...  65.5 us
    dot_general x1, matrix products, local_step(): jnp.einsum('bths,bsc->bthc', weights.astype(jnp.bfloat16), local_keys[:,...  48.7 us
    convert_element_type x1, local copies, waits for them, and re-layouts, local_step(): part_out = (part_out / row_sum[..., None]).astype(jnp.bfloat16)  24.5 us
    reduce_sum x1, other arithmetic, local_step(): merged = jnp.sum(merge_w[..., None] * recv_out.astype(jnp.float32), axis=2)  24 us
    reduce_sum x1, other arithmetic, local_step(): row_sum = jnp.sum(weights, axis=-1)  21.5 us
  transfers between devices with their start and end apart: 3, of which 2 were waited for; matrix products, arithmetic and copies ran while one was open for 16% of the time, Pallas kernels for 0%

commit v1 on v0

v1 whole, which is shorter than its diff:
```python
import functools
import math

import jax
import jax.numpy as jnp
from jax import lax
from jax.experimental import pallas as pl
from jax.experimental.pallas import tpu as pltpu
from jax.sharding import PartitionSpec as P

LATENT = 512
ROPE = 64
NOPE = 128
PAGE = 64
CORES = 2
SCALE2 = (NOPE + ROPE) ** -0.5 * math.log2(math.e)

GQ = 4
GO = 8
KV_SLOTS = 4
AHEAD = 3
HOLD = 13


def _kernel(sizes, q_hbm, kv_hbm, len_ref, out_hbm,
            qall, rope_in, kvb, o_all, prx, abuf, bbuf,
            lse_all, plse, clse, alse, nlse, blse, wt,
            load_sem, kv_sem, out_sem, qs, qr, ds, dr, as_, ar, bs, br):
    batch, toks, heads, npos, group = sizes
    chips = group // CORES
    rows = toks * heads
    half = GO // 2
    n_q, n_o = batch // GQ, batch // GO
    me = lax.axis_index('dcp')
    c, k = me // CORES, me % CORES
    ok = 1 - k
    cr, cl, cf = (c + 1) % chips, (c + chips - 1) % chips, (c + 2) % chips
    right, left, partner = cr * CORES + k, cl * CORES + k, c * CORES + ok

    barrier = pltpu.get_barrier_semaphore()
    for other in (right, left, partner):
        pl.semaphore_signal(barrier, inc=1, device_id={'dcp': other}, device_id_type=pl.DeviceIdType.MESH)

    def rcopy(src, dst, send, recv, dev):
        return pltpu.make_async_remote_copy(src_ref=src, dst_ref=dst, send_sem=send, recv_sem=recv,
                                            device_id={'dcp': dev}, device_id_type=pl.DeviceIdType.MESH)

    loads = [pltpu.make_async_copy(q_hbm.at[:, t, :, 0:LATENT], qall.at[k, c, :, :, t * LATENT:(t + 1) * LATENT], load_sem.at[t])
             for t in range(toks)]
    loads.append(pltpu.make_async_copy(q_hbm.at[:, :, :, LATENT:LATENT + ROPE], rope_in, load_sem.at[toks]))
    for cp in loads:
        cp.start()

    def kv_copy(b):
        slot = lax.rem(b, KV_SLOTS)
        return pltpu.make_async_copy(kv_hbm.at[b], kvb.at[slot], kv_sem.at[slot])

    for b in range(KV_SLOTS):
        kv_copy(b).start()
    loads[toks].wait()

    def pack(b, carry):
        both = [rope_in[b, t] for t in range(toks)]
        qall[k, c, b, :, toks * LATENT:] = jnp.concatenate(both, axis=-1)
        return carry

    lax.fori_loop(0, batch, pack, 0)
    for t in range(toks):
        loads[t].wait()
    pl.semaphore_wait(barrier, 3)

    def qreg(kk, cc, b0, n):
        return qall.at[kk, cc, pl.ds(b0, n)]

    def q_own(j):
        r = qreg(k, c, j * GQ, GQ)
        return [rcopy(r, r, qs.at[0, j], qr.at[0, j], right), rcopy(r, r, qs.at[1, j], qr.at[1, j], left),
                rcopy(r, r, qs.at[2, j], qr.at[2, j], partner)]

    def q_relay(j):
        lr, rr = qreg(k, cl, j * GQ, GQ), qreg(k, cr, j * GQ, GQ)
        lh, rh = qreg(k, cl, j * GQ, GQ // 2), qreg(k, cr, j * GQ + GQ // 2, GQ // 2)
        return [rcopy(lh, lh, qs.at[3, j], qr.at[3, j], right), rcopy(rh, rh, qs.at[4, j], qr.at[4, j], left),
                rcopy(lr, lr, qs.at[5, j], qr.at[5, j], partner), rcopy(rr, rr, qs.at[6, j], qr.at[6, j], partner)]

    def q_far(j):
        f0, f1 = qreg(k, cf, j * GQ, GQ // 2), qreg(k, cf, j * GQ + GQ // 2, GQ // 2)
        return [rcopy(f0, f0, qs.at[7, j], qr.at[7, j], partner), rcopy(f1, f1, qs.at[8, j], qr.at[8, j], partner)]

    def q_arrival(kind, j):
        full, h0, h1 = (j * GQ, GQ), (j * GQ, GQ // 2), (j * GQ + GQ // 2, GQ // 2)
        kk, cc, span = [(k, cl, full), (k, cr, full), (ok, c, full), (k, cf, h0), (k, cf, h1),
                        (ok, cl, full), (ok, cr, full), (ok, cf, h0), (ok, cf, h1)][kind]
        r = qreg(kk, cc, *span)
        return rcopy(r, r, qs.at[kind, j], qr.at[kind, j], partner)

    row_tok = (lax.broadcasted_iota(jnp.int32, (CORES * chips * rows, 1), 0) // heads) % toks
    key = lax.broadcasted_iota(jnp.int32, (1, npos), 1)
    pos = ((key // PAGE) * group + me) * PAGE + key % PAGE
    lanes = chips * rows
    eye = lax.broadcasted_iota(jnp.int32, (lanes, lanes), 0) == lax.broadcasted_iota(jnp.int32, (lanes, lanes), 1)

    def attend(b):
        kv_copy(b).wait()
        slot = lax.rem(b, KV_SLOTS)
        q = qall[:, :, b].reshape(CORES * chips, heads, toks * (LATENT + ROPE))
        lat = jnp.stack([q[:, :, t * LATENT:(t + 1) * LATENT] for t in range(toks)], axis=1).reshape(-1, LATENT)
        rope0 = toks * LATENT
        rope = jnp.stack([q[:, :, rope0 + t * ROPE:rope0 + (t + 1) * ROPE] for t in range(toks)], axis=1).reshape(-1, ROPE)
        q_rows = jnp.concatenate([lat, rope], axis=-1)
        s = lax.dot_general(q_rows, kvb[slot], (((1,), (1,)), ((), ())), preferred_element_type=jnp.float32)
        s = jnp.where(pos <= len_ref[b] - toks + row_tok, s, -jnp.inf)
        m = jnp.max(s, axis=-1, keepdims=True)
        p = jnp.exp2((s - m) * SCALE2)
        l = jnp.sum(p, axis=-1, keepdims=True)
        o = jnp.dot(p.astype(jnp.bfloat16), kvb[slot, :, 0:LATENT], preferred_element_type=jnp.float32)
        o = (o * (1.0 / l)).astype(jnp.bfloat16)
        o_all[:, :, b] = o.reshape(CORES, chips, rows, LATENT)
        lse = m * SCALE2 + jnp.log2(l)
        for kk in range(CORES):
            col = lse[kk * lanes:(kk + 1) * lanes]
            lse_all[kk, pl.ds(b, 1)] = jnp.sum(jnp.where(eye, col, 0.0), axis=0, keepdims=True)

        @pl.when(b + KV_SLOTS < batch)
        def _():
            kv_copy(b + KV_SLOTS).start()

    def seqs(i, n=GO):
        return pl.ds(pl.multiple_of(i * n, n), n)

    def d_send(i):
        return [rcopy(o_all.at[ok, :, seqs(i)], prx.at[:, seqs(i)], ds.at[0, i], dr.at[0, i], partner),
                rcopy(lse_all.at[ok, seqs(i)], plse.at[seqs(i)], ds.at[1, i], dr.at[1, i], partner)]

    def d_merge(i):
        for cp in d_send(i):
            cp.wait_recv()
        a, b = lse_all[k, seqs(i)], plse[seqs(i)]
        top = jnp.maximum(a, b)
        both = top + jnp.log2(jnp.exp2(a - top) + jnp.exp2(b - top))
        clse[seqs(i)] = both
        wa, wb = jnp.transpose(jnp.exp2(a - both)), jnp.transpose(jnp.exp2(b - both))
        for j in range(GO):
            for cc in range(chips):
                sl = slice(cc * rows, (cc + 1) * rows)
                x = o_all[k, cc, i * GO + j].astype(jnp.float32) * wa[sl, j:j + 1]
                y = prx[cc, i * GO + j].astype(jnp.float32) * wb[sl, j:j + 1]
                o_all[k, cc, i * GO + j] = (x + y).astype(jnp.bfloat16)

    def oreg(cc, i, part):
        if part is None:
            return o_all.at[k, cc, seqs(i)]
        return o_all.at[k, cc, pl.ds(i * GO + part * half, half)]

    def breg(side, i, part):
        return bbuf.at[side, pl.ds(i * GO + part * half, half)]

    def a_send(i):
        return [rcopy(oreg(cf, i, 0), abuf.at[0, pl.ds(i * half, half)], as_.at[0, i], ar.at[0, i], right),
                rcopy(oreg(cf, i, 1), abuf.at[1, pl.ds(i * half, half)], as_.at[1, i], ar.at[1, i], left),
                rcopy(clse.at[seqs(i)], alse.at[0, seqs(i)], as_.at[2, i], ar.at[2, i], right),
                rcopy(clse.at[seqs(i)], alse.at[1, seqs(i)], as_.at[3, i], ar.at[3, i], left)]

    def b_early(i):
        return [rcopy(oreg(cr, i, 1), breg(0, i, 1), bs.at[0, i], br.at[0, i], right),
                rcopy(oreg(cl, i, 0), breg(1, i, 0), bs.at[1, i], br.at[1, i], left)]

    def b_late(i):
        return [rcopy(oreg(cr, i, 0), breg(0, i, 0), bs.at[2, i], br.at[2, i], right),
                rcopy(oreg(cl, i, 1), breg(1, i, 1), bs.at[3, i], br.at[3, i], left),
                rcopy(nlse.at[seqs(i)], blse.at[0, seqs(i)], bs.at[4, i], br.at[4, i], right),
                rcopy(nlse.at[seqs(i)], blse.at[1, seqs(i)], bs.at[5, i], br.at[5, i], left)]

    seq_id = lax.broadcasted_iota(jnp.int32, (GO, lanes), 0)
    chip_id = lax.broadcasted_iota(jnp.int32, (GO, lanes), 1) // rows
    from_left = (seq_id < half) & (chip_id == cr)
    from_right = (seq_id >= half) & (chip_id == cl)

    def a_merge(i):
        for cp in a_send(i):
            cp.wait_recv()
        a = clse[seqs(i)]
        b = jnp.where(from_left, alse[0, seqs(i)], jnp.where(from_right, alse[1, seqs(i)], a))
        top = jnp.maximum(a, b)
        both = top + jnp.log2(jnp.exp2(a - top) + jnp.exp2(b - top))
        wt[0], wt[1] = jnp.transpose(jnp.exp2(a - both)), jnp.transpose(jnp.exp2(b - both))
        nlse[seqs(i)] = jnp.where(from_left | from_right, both, a)
        for side, cc in ((0, cr), (1, cl)):
            wa, wb = (wt[n, pl.ds(pl.multiple_of(cc * rows, rows), rows)] for n in range(2))
            for j in range(half):
                lane = side * half + j
                x = o_all[k, cc, i * GO + lane].astype(jnp.float32) * wa[:, lane:lane + 1]
                y = abuf[side, i * half + j].astype(jnp.float32) * wb[:, lane:lane + 1]
                o_all[k, cc, i * GO + lane] = (x + y).astype(jnp.bfloat16)
        for cp in b_late(i):
            cp.start()

    def out_copy(i):
        return pltpu.make_async_copy(o_all.at[k, c, seqs(i)], out_hbm.at[seqs(i)], out_sem.at[i])

    def final_merge(i):
        for cp in b_early(i) + b_late(i):
            cp.wait_recv()
        parts = [clse[seqs(i)], blse[0, seqs(i)], blse[1, seqs(i)]]
        top = functools.reduce(jnp.maximum, parts)
        total = top + jnp.log2(sum(jnp.exp2(x - top) for x in parts))
        for n, x in enumerate(parts):
            wt[n] = jnp.transpose(jnp.exp2(x - total))
        w = [wt[n, pl.ds(pl.multiple_of(c * rows, rows), rows)] for n in range(3)]
        for j in range(GO):
            b = i * GO + j
            x = o_all[k, c, b].astype(jnp.float32) * w[0][:, j:j + 1]
            x += bbuf[0, b].astype(jnp.float32) * w[1][:, j:j + 1]
            x += bbuf[1, b].astype(jnp.float32) * w[2][:, j:j + 1]
            o_all[k, c, b] = x.astype(jnp.bfloat16)
        out_copy(i).start()

    def ring_start(i):
        for cp in a_send(i) + b_early(i):
            cp.start()

    for j in range(AHEAD):
        for cp in q_own(j):
            cp.start()

    def step(j, carry):
        @pl.when(j < n_q)
        def _():
            q_arrival(0, j).wait_recv()
            q_arrival(1, j).wait_recv()
            for cp in q_relay(j):
                cp.start()

        @pl.when(j + AHEAD < n_q)
        def _():
            for cp in q_own(j + AHEAD):
                cp.start()

        @pl.when((j >= 1) & (j <= n_q))
        def _():
            q_arrival(3, j - 1).wait_recv()
            q_arrival(4, j - 1).wait_recv()
            for cp in q_far(j - 1):
                cp.start()

        @pl.when(j == HOLD)
        def _():
            lax.fori_loop(0, (HOLD - 3) // 2, lambda i, cc: (ring_start(i), cc)[1], 0)

        @pl.when(j >= 2)
        def _():
            s = j - 2
            for kind in (2, 5, 6, 7, 8):
                q_arrival(kind, s).wait_recv()
            lax.fori_loop(0, GQ, lambda n, cc: (attend(s * GQ + n), cc)[1], 0)
            i = s // 2

            @pl.when(s % 2 == 1)
            def _():
                for cp in d_send(i):
                    cp.start()

            @pl.when((s % 2 == 0) & (s > 0))
            def _():
                d_merge(i - 1)

                @pl.when(j >= HOLD)
                def _():
                    ring_start(i - 1)

        return carry

    lax.fori_loop(0, n_q + 2, step, 0)
    d_merge(n_o - 1)
    ring_start(n_o - 1)
    lax.fori_loop(0, n_o, lambda i, cc: (a_merge(i), cc)[1], 0)
    lax.fori_loop(0, n_o, lambda i, cc: (final_merge(i), cc)[1], 0)

    def drain_q(j, carry):
        for cp in q_own(j) + q_relay(j) + q_far(j):
            cp.wait_send()
        return carry

    def drain_o(i, carry):
        for cp in d_send(i) + a_send(i) + b_early(i) + b_late(i):
            cp.wait_send()
        out_copy(i).wait()
        return carry

    lax.fori_loop(0, n_q, drain_q, 0)
    lax.fori_loop(0, n_o, drain_o, 0)


def solution(mesh):
    group = mesh.shape['dcp']
    chips = group // CORES

    def local_step(q_blk, kv_blk, len_blk):
        batch, toks, heads, width = q_blk.shape
        npos = kv_blk.shape[1] * kv_blk.shape[2] * kv_blk.shape[3]
        rows, lanes = toks * heads, chips * toks * heads
        n_q, n_o = batch // GQ, batch // GO
        bf16, f32, dma = jnp.bfloat16, jnp.float32, pltpu.SemaphoreType.DMA
        any_space = pl.BlockSpec(memory_space=pl.ANY)
        out = pl.pallas_call(
            functools.partial(_kernel, (batch, toks, heads, npos, group)),
            out_shape=jax.ShapeDtypeStruct((batch, rows, LATENT), bf16),
            in_specs=[any_space, any_space, pl.BlockSpec(memory_space=pltpu.SMEM)],
            out_specs=any_space,
            scratch_shapes=[
                pltpu.VMEM((CORES, chips, batch, heads, toks * width), bf16),
                pltpu.VMEM((batch, toks, heads, ROPE), bf16),
                pltpu.VMEM((KV_SLOTS, npos, width), bf16),
                pltpu.VMEM((CORES, chips, batch, rows, LATENT), bf16),
                pltpu.VMEM((chips, batch, rows, LATENT), bf16),
                pltpu.VMEM((2, batch // 2, rows, LATENT), bf16),
                pltpu.VMEM((2, batch, rows, LATENT), bf16),
                pltpu.VMEM((CORES, batch, lanes), f32),
                pltpu.VMEM((batch, lanes), f32),
                pltpu.VMEM((batch, lanes), f32),
                pltpu.VMEM((2, batch, lanes), f32),
                pltpu.VMEM((batch, lanes), f32),
                pltpu.VMEM((2, batch, lanes), f32),
                pltpu.VMEM((3, lanes, GO), f32),
                dma((toks + 1,)), dma((KV_SLOTS,)), dma((n_o,)),
                dma((9, n_q)), dma((9, n_q)),
                dma((2, n_o)), dma((2, n_o)),
                dma((4, n_o)), dma((4, n_o)),
                dma((6, n_o)), dma((6, n_o)),
            ],
            compiler_params=pltpu.CompilerParams(collective_id=0, has_side_effects=True, vmem_limit_bytes=67_043_328),
            name='mla_ring',
        )(q_blk, kv_blk.reshape(batch, npos, width), len_blk)
        return out.reshape(batch, toks, heads, LATENT)

    return jax.shard_map(local_step, mesh=mesh, in_specs=(P('dp', None, 'dcp', None), P('dp', None, 'dcp', None, None), P('dp')),
                         out_specs=P('dp', None, 'dcp', None), check_vma=False)
```

time: 501 us -> 175 us (0.35)
  waiting for transfers between devices: 283 us -> 0 us
  Pallas kernels: 0 us -> 170 us
  matrix products: 114 us -> 0 us
  other arithmetic: 47.6 us -> 0 us
  local copies, waits for them, and re-layouts: 32.4 us -> 3.22 us
  between operations: 13.5 us -> 0.01 us
  starting transfers between devices: 9.89 us -> 0 us
    all_to_all x2 -> x0, waiting for transfers between devices: 180 us -> none  [the longest x1 180 us: local_step(): lax.all_to_all(part_out, 'dcp', 2, 2, tiled=True)]
    pallas_call x0 -> x1, Pallas kernels: none -> 170 us  [local_step(): pl.pallas_call(functools.partial(_kernel, (batch, toks, heads, npos, grou...]
    dot_general x2 -> x0, matrix products: 114 us -> none  [the longest x1 65.5 us: local_step(): jnp.einsum('bthd,bsd->bths', q_all, local_keys, preferred_element_type=jn...]
    all_gather x1 -> x0, waiting for transfers between devices: 102 us -> none  [local_step(): q_all = lax.all_gather(q_blk, 'dcp', axis=2, tiled=True)]
    reduce_sum x3 -> x0, other arithmetic: 45.5 us -> none  [the longest x1 24 us: local_step(): merged = jnp.sum(merge_w[..., None] * recv_out.astype(jnp.float32), axis=2)]
    convert_element_type x2 -> x0, local copies, waits for them, and re-layouts: 28 us -> none  [the longest x1 24.5 us: local_step(): part_out = (part_out / row_sum[..., None]).astype(jnp.bfloat16)]
    all_to_all x2 -> x0, starting transfers between devices: 9.89 us -> none  [the longest x1 6.13 us: local_step(): lax.all_to_all(part_out, 'dcp', 2, 2, tiled=True)]
  transfers between devices with their start and end apart: 3 -> 0, of which waited for: 2 -> 0; matrix products, arithmetic and copies ran while one was open for 16% -> 0% of each run, Pallas kernels for 0% -> 0%
where the time goes in v1:
time: 175 us; the launch traced here: 173 us
  Pallas kernels  170 us (97%)
  local copies, waits for them, and re-layouts  3.22 us (2%)
    pallas_call x1, Pallas kernels, local_step(): pl.pallas_call(functools.partial(_kernel, (batch, toks, heads, npos, grou...  170 us

profile of v1, /device:TPU:112, one launch (start us, length us, event | category | flops | bytes accessed | tf_op | source)
XLA Modules:
  0.0 173.1 jit_solution(2050994591865730606)
XLA Ops:
  0.0 169.8 %mla_ring.1 = bf16[64,32,512]{2,1,0:T(8,128)(2,1)} custom-call(bf16[64,2,16,576]{3,2,1,0:T(8,128)(2,1)} %q_hbm.1, bf16[64,1024,576]{2,1,0:T(8,128)(2,1)} %bitcast.kv_hbm, s32[64]{0:T(128)} %len_ref.1), custom_call_target="tpu_custom_call" | custom-call | tf_op jit(solution)/shard_map/mla_ring/pallas_call | solution.py:305
  169.9 3.2 %copy.5 = bf16[64,2,16,512]{3,2,1,0:T(8,128)(2,1)} copy(bf16[64,2,16,512]{3,2,1,0:T(8,128)(2,1)} %bitcast.2) | data formatting | bytes 4194304

commit v2 on v1

--- a/solution.py
+++ b/solution.py
@@ -18,8 +18,8 @@
 GQ = 4
 GO = 8
 KV_SLOTS = 4
-AHEAD = 3
-HOLD = 13
+UNROLL = 2
+AHEAD = 2
 
 
 def _kernel(sizes, q_hbm, kv_hbm, len_ref, out_hbm,
@@ -48,26 +48,17 @@
     loads = [pltpu.make_async_copy(q_hbm.at[:, t, :, 0:LATENT], qall.at[k, c, :, :, t * LATENT:(t + 1) * LATENT], load_sem.at[t])
              for t in range(toks)]
     loads.append(pltpu.make_async_copy(q_hbm.at[:, :, :, LATENT:LATENT + ROPE], rope_in, load_sem.at[toks]))
-    for cp in loads:
+    for cp in loads[::-1]:
         cp.start()
+    loads[toks].wait()
+    qall[k, c, :, :, toks * LATENT:] = jnp.concatenate([rope_in[:, t] for t in range(toks)], axis=-1)
+    for t in range(toks):
+        loads[t].wait()
+    pl.semaphore_wait(barrier, 3)
 
     def kv_copy(b):
         slot = lax.rem(b, KV_SLOTS)
         return pltpu.make_async_copy(kv_hbm.at[b], kvb.at[slot], kv_sem.at[slot])
-
-    for b in range(KV_SLOTS):
-        kv_copy(b).start()
-    loads[toks].wait()
-
-    def pack(b, carry):
-        both = [rope_in[b, t] for t in range(toks)]
-        qall[k, c, b, :, toks * LATENT:] = jnp.concatenate(both, axis=-1)
-        return carry
-
-    lax.fori_loop(0, batch, pack, 0)
-    for t in range(toks):
-        loads[t].wait()
-    pl.semaphore_wait(barrier, 3)
 
     def qreg(kk, cc, b0, n):
         return qall.at[kk, cc, pl.ds(b0, n)]
@@ -100,7 +91,7 @@
     lanes = chips * rows
     eye = lax.broadcasted_iota(jnp.int32, (lanes, lanes), 0) == lax.broadcasted_iota(jnp.int32, (lanes, lanes), 1)
 
-    def attend(b):
+    def scores(b):
         kv_copy(b).wait()
         slot = lax.rem(b, KV_SLOTS)
         q = qall[:, :, b].reshape(CORES * chips, heads, toks * (LATENT + ROPE))
@@ -108,12 +99,17 @@
         rope0 = toks * LATENT
         rope = jnp.stack([q[:, :, rope0 + t * ROPE:rope0 + (t + 1) * ROPE] for t in range(toks)], axis=1).reshape(-1, ROPE)
         q_rows = jnp.concatenate([lat, rope], axis=-1)
-        s = lax.dot_general(q_rows, kvb[slot], (((1,), (1,)), ((), ())), preferred_element_type=jnp.float32)
+        return lax.dot_general(q_rows, kvb[slot], (((1,), (1,)), ((), ())), preferred_element_type=jnp.float32)
+
+    def weights(b, s):
         s = jnp.where(pos <= len_ref[b] - toks + row_tok, s, -jnp.inf)
         m = jnp.max(s, axis=-1, keepdims=True)
         p = jnp.exp2((s - m) * SCALE2)
-        l = jnp.sum(p, axis=-1, keepdims=True)
-        o = jnp.dot(p.astype(jnp.bfloat16), kvb[slot, :, 0:LATENT], preferred_element_type=jnp.float32)
+        return m, jnp.sum(p, axis=-1, keepdims=True), p.astype(jnp.bfloat16)
+
+    def output(b, m, l, p):
+        slot = lax.rem(b, KV_SLOTS)
+        o = jnp.dot(p, kvb[slot, :, 0:LATENT], preferred_element_type=jnp.float32)
         o = (o * (1.0 / l)).astype(jnp.bfloat16)
         o_all[:, :, b] = o.reshape(CORES, chips, rows, LATENT)
         lse = m * SCALE2 + jnp.log2(l)
@@ -121,9 +117,15 @@
             col = lse[kk * lanes:(kk + 1) * lanes]
             lse_all[kk, pl.ds(b, 1)] = jnp.sum(jnp.where(eye, col, 0.0), axis=0, keepdims=True)
 
-        @pl.when(b + KV_SLOTS < batch)
-        def _():
-            kv_copy(b + KV_SLOTS).start()
+    def attend(b0):
+        bs_ = [b0 + u for u in range(UNROLL)]
+        ss = [scores(b) for b in bs_]
+        for b, s in zip(bs_, ss):
+            output(b, *weights(b, s))
+        for b in bs_:
+            @pl.when(b + KV_SLOTS < batch)
+            def _():
+                kv_copy(b + KV_SLOTS).start()
 
     def seqs(i, n=GO):
         return pl.ds(pl.multiple_of(i * n, n), n)
@@ -215,13 +217,18 @@
             o_all[k, c, b] = x.astype(jnp.bfloat16)
         out_copy(i).start()
 
-    def ring_start(i):
-        for cp in a_send(i) + b_early(i):
+    def start(copies):
+        for cp in copies:
             cp.start()
+
+    def ring_start(lo, hi):
+        lax.fori_loop(lo, hi, lambda i, carry: (start(a_send(i) + b_early(i)), carry)[1], 0)
 
     for j in range(AHEAD):
         for cp in q_own(j):
             cp.start()
+    for b in range(KV_SLOTS):
+        kv_copy(b).start()
 
     def step(j, carry):
         @pl.when(j < n_q)
@@ -243,16 +250,29 @@
             for cp in q_far(j - 1):
                 cp.start()
 
-        @pl.when(j == HOLD)
-        def _():
-            lax.fori_loop(0, (HOLD - 3) // 2, lambda i, cc: (ring_start(i), cc)[1], 0)
+        @pl.when(j == n_q - 2)
+        def _():
+            start(a_send(0))
+
+        @pl.when(j == n_q - 1)
+        def _():
+            start(b_early(0))
+            ring_start(1, n_o // 2)
+
+        @pl.when(j == n_q)
+        def _():
+            ring_start(n_o // 2, n_o - 2)
+
+        @pl.when(j == n_q + 1)
+        def _():
+            ring_start(n_o - 2, n_o - 1)
 
         @pl.when(j >= 2)
         def _():
             s = j - 2
             for kind in (2, 5, 6, 7, 8):
                 q_arrival(kind, s).wait_recv()
-            lax.fori_loop(0, GQ, lambda n, cc: (attend(s * GQ + n), cc)[1], 0)
+            lax.fori_loop(0, GQ // UNROLL, lambda n, cc: (attend(s * GQ + n * UNROLL), cc)[1], 0)
             i = s // 2
 
             @pl.when(s % 2 == 1)
@@ -264,15 +284,11 @@
             def _():
                 d_merge(i - 1)
 
-                @pl.when(j >= HOLD)
-                def _():
-                    ring_start(i - 1)
-
         return carry
 
     lax.fori_loop(0, n_q + 2, step, 0)
     d_merge(n_o - 1)
-    ring_start(n_o - 1)
+    ring_start(n_o - 1, n_o)
     lax.fori_loop(0, n_o, lambda i, cc: (a_merge(i), cc)[1], 0)
     lax.fori_loop(0, n_o, lambda i, cc: (final_merge(i), cc)[1], 0)
 

time: 175 us -> 161 us (0.920)
  Pallas kernels: 170 us -> 157 us
    pallas_call x1, Pallas kernels: 170 us -> 157 us  [local_step(): pl.pallas_call(functools.partial(_kernel, (batch, toks, heads, npos, grou...]
where the time goes in v2:
time: 161 us
  Pallas kernels  157 us (98%)
  local copies, waits for them, and re-layouts  3.22 us (2%)
    pallas_call x1, Pallas kernels, local_step(): pl.pallas_call(functools.partial(_kernel, (batch, toks, heads, npos, grou...  157 us
    unnamed x1, local copies, waits for them, and re-layouts  3.22 us

profile of v2, /device:TPU:112, one launch (start us, length us, event | category | flops | bytes accessed | tf_op | source)
XLA Modules:
  0.0 160.6 jit_solution(12995058772033617275)
XLA Ops:
  0.0 157.4 %mla_ring.1 = bf16[64,32,512]{2,1,0:T(8,128)(2,1)} custom-call(bf16[64,2,16,576]{3,2,1,0:T(8,128)(2,1)} %q_hbm.1, bf16[64,1024,576]{2,1,0:T(8,128)(2,1)} %bitcast.kv_hbm, s32[64]{0:T(128)} %len_ref.1), custom_call_target="tpu_custom_call" | custom-call | tf_op jit(solution)/shard_map/mla_ring/pallas_call | solution.py:321
  157.4 3.2 %copy.5 = bf16[64,2,16,512]{3,2,1,0:T(8,128)(2,1)} copy(bf16[64,2,16,512]{3,2,1,0:T(8,128)(2,1)} %bitcast.2) | data formatting | bytes 4194304

commit v3 on v2

--- a/solution.py
+++ b/solution.py
@@ -22,10 +22,10 @@
 AHEAD = 2
 
 
-def _kernel(sizes, q_hbm, kv_hbm, len_ref, out_hbm,
+def _kernel(sizes, q_hbm, kv_hbm, len_ref, out_ref,
             qall, rope_in, kvb, o_all, prx, abuf, bbuf,
             lse_all, plse, clse, alse, nlse, blse, wt,
-            load_sem, kv_sem, out_sem, qs, qr, ds, dr, as_, ar, bs, br):
+            load_sem, kv_sem, qs, qr, ds, dr, as_, ar, bs, br):
     batch, toks, heads, npos, group = sizes
     chips = group // CORES
     rows = toks * heads
@@ -45,16 +45,29 @@
         return pltpu.make_async_remote_copy(src_ref=src, dst_ref=dst, send_sem=send, recv_sem=recv,
                                             device_id={'dcp': dev}, device_id_type=pl.DeviceIdType.MESH)
 
-    loads = [pltpu.make_async_copy(q_hbm.at[:, t, :, 0:LATENT], qall.at[k, c, :, :, t * LATENT:(t + 1) * LATENT], load_sem.at[t])
-             for t in range(toks)]
-    loads.append(pltpu.make_async_copy(q_hbm.at[:, :, :, LATENT:LATENT + ROPE], rope_in, load_sem.at[toks]))
-    for cp in loads[::-1]:
-        cp.start()
-    loads[toks].wait()
-    qall[k, c, :, :, toks * LATENT:] = jnp.concatenate([rope_in[:, t] for t in range(toks)], axis=-1)
-    for t in range(toks):
-        loads[t].wait()
-    pl.semaphore_wait(barrier, 3)
+    spans = ((0, AHEAD * GQ), (AHEAD * GQ, batch))
+
+    def q_loads(n):
+        span = slice(*spans[n])
+        lat = [pltpu.make_async_copy(q_hbm.at[span, t, :, 0:LATENT], qall.at[k, c, span, :, t * LATENT:(t + 1) * LATENT], load_sem.at[n, t])
+               for t in range(toks)]
+        return lat, pltpu.make_async_copy(q_hbm.at[span, :, :, LATENT:LATENT + ROPE], rope_in.at[span], load_sem.at[n, toks])
+
+    def q_ready(n):
+        lat, rope = q_loads(n)
+        span = slice(*spans[n])
+        rope.wait()
+        qall[k, c, span, :, toks * LATENT:] = jnp.concatenate([rope_in[span, t] for t in range(toks)], axis=-1)
+        for cp in lat:
+            cp.wait()
+
+    def start(copies):
+        for cp in copies:
+            cp.start()
+
+    for n in range(2):
+        lat, rope = q_loads(n)
+        start([rope] + lat)
 
     def kv_copy(b):
         slot = lax.rem(b, KV_SLOTS)
@@ -92,7 +105,6 @@
     eye = lax.broadcasted_iota(jnp.int32, (lanes, lanes), 0) == lax.broadcasted_iota(jnp.int32, (lanes, lanes), 1)
 
     def scores(b):
-        kv_copy(b).wait()
         slot = lax.rem(b, KV_SLOTS)
         q = qall[:, :, b].reshape(CORES * chips, heads, toks * (LATENT + ROPE))
         lat = jnp.stack([q[:, :, t * LATENT:(t + 1) * LATENT] for t in range(toks)], axis=1).reshape(-1, LATENT)
@@ -119,9 +131,13 @@
 
     def attend(b0):
         bs_ = [b0 + u for u in range(UNROLL)]
-        ss = [scores(b) for b in bs_]
-        for b, s in zip(bs_, ss):
+        for b in bs_:
+            kv_copy(b).wait()
+        s = scores(bs_[0])
+        for b in bs_:
+            following = scores(b + 1) if b is not bs_[-1] else None
             output(b, *weights(b, s))
+            s = following
         for b in bs_:
             @pl.when(b + KV_SLOTS < batch)
             def _():
@@ -194,15 +210,12 @@
                 x = o_all[k, cc, i * GO + lane].astype(jnp.float32) * wa[:, lane:lane + 1]
                 y = abuf[side, i * half + j].astype(jnp.float32) * wb[:, lane:lane + 1]
                 o_all[k, cc, i * GO + lane] = (x + y).astype(jnp.bfloat16)
-        for cp in b_late(i):
-            cp.start()
-
-    def out_copy(i):
-        return pltpu.make_async_copy(o_all.at[k, c, seqs(i)], out_hbm.at[seqs(i)], out_sem.at[i])
+        start(b_late(i))
 
     def final_merge(i):
         for cp in b_early(i) + b_late(i):
             cp.wait_recv()
+        sent(b_late(i))
         parts = [clse[seqs(i)], blse[0, seqs(i)], blse[1, seqs(i)]]
         top = functools.reduce(jnp.maximum, parts)
         total = top + jnp.log2(sum(jnp.exp2(x - top) for x in parts))
@@ -214,21 +227,22 @@
             x = o_all[k, c, b].astype(jnp.float32) * w[0][:, j:j + 1]
             x += bbuf[0, b].astype(jnp.float32) * w[1][:, j:j + 1]
             x += bbuf[1, b].astype(jnp.float32) * w[2][:, j:j + 1]
-            o_all[k, c, b] = x.astype(jnp.bfloat16)
-        out_copy(i).start()
-
-    def start(copies):
+            out_ref[b] = x.astype(jnp.bfloat16)
+
+    def sent(copies):
         for cp in copies:
-            cp.start()
+            cp.wait_send()
 
     def ring_start(lo, hi):
         lax.fori_loop(lo, hi, lambda i, carry: (start(a_send(i) + b_early(i)), carry)[1], 0)
 
+    q_ready(0)
+    pl.semaphore_wait(barrier, 3)
     for j in range(AHEAD):
-        for cp in q_own(j):
-            cp.start()
+        start(q_own(j))
     for b in range(KV_SLOTS):
         kv_copy(b).start()
+    q_ready(1)
 
     def step(j, carry):
         @pl.when(j < n_q)
@@ -289,22 +303,10 @@
     lax.fori_loop(0, n_q + 2, step, 0)
     d_merge(n_o - 1)
     ring_start(n_o - 1, n_o)
+    lax.fori_loop(0, n_q, lambda j, cc: (sent(q_own(j) + q_relay(j) + q_far(j)), cc)[1], 0)
     lax.fori_loop(0, n_o, lambda i, cc: (a_merge(i), cc)[1], 0)
+    lax.fori_loop(0, n_o, lambda i, cc: (sent(d_send(i) + a_send(i) + b_early(i)), cc)[1], 0)
     lax.fori_loop(0, n_o, lambda i, cc: (final_merge(i), cc)[1], 0)
-
-    def drain_q(j, carry):
-        for cp in q_own(j) + q_relay(j) + q_far(j):
-            cp.wait_send()
-        return carry
-
-    def drain_o(i, carry):
-        for cp in d_send(i) + a_send(i) + b_early(i) + b_late(i):
-            cp.wait_send()
-        out_copy(i).wait()
-        return carry
-
-    lax.fori_loop(0, n_q, drain_q, 0)
-    lax.fori_loop(0, n_o, drain_o, 0)
 
 
 def solution(mesh):
@@ -320,9 +322,9 @@
         any_space = pl.BlockSpec(memory_space=pl.ANY)
         out = pl.pallas_call(
             functools.partial(_kernel, (batch, toks, heads, npos, group)),
-            out_shape=jax.ShapeDtypeStruct((batch, rows, LATENT), bf16),
+            out_shape=pltpu.VMEM((batch, rows, LATENT), bf16),
             in_specs=[any_space, any_space, pl.BlockSpec(memory_space=pltpu.SMEM)],
-            out_specs=any_space,
+            out_specs=pl.BlockSpec(memory_space=pltpu.VMEM),
             scratch_shapes=[
                 pltpu.VMEM((CORES, chips, batch, heads, toks * width), bf16),
                 pltpu.VMEM((batch, toks, heads, ROPE), bf16),
@@ -338,13 +340,13 @@
                 pltpu.VMEM((batch, lanes), f32),
                 pltpu.VMEM((2, batch, lanes), f32),
                 pltpu.VMEM((3, lanes, GO), f32),
-                dma((toks + 1,)), dma((KV_SLOTS,)), dma((n_o,)),
+                dma((2, toks + 1)), dma((KV_SLOTS,)),
                 dma((9, n_q)), dma((9, n_q)),
                 dma((2, n_o)), dma((2, n_o)),
                 dma((4, n_o)), dma((4, n_o)),
                 dma((6, n_o)), dma((6, n_o)),
             ],
-            compiler_params=pltpu.CompilerParams(collective_id=0, has_side_effects=True, vmem_limit_bytes=67_043_328),
+            compiler_params=pltpu.CompilerParams(collective_id=0, has_side_effects=True, vmem_limit_bytes=63_000_000),
             name='mla_ring',
         )(q_blk, kv_blk.reshape(batch, npos, width), len_blk)
         return out.reshape(batch, toks, heads, LATENT)

time: 161 us -> 157 us (0.975)
  local copies, waits for them, and re-layouts: 3.22 us -> 1.32 us
    unnamed x1, local copies, waits for them, and re-layouts: 3.22 us -> 1.32 us
where the time goes in v3:
time: 157 us
  Pallas kernels  156 us (99%)
    pallas_call x1, Pallas kernels, local_step(): pl.pallas_call(functools.partial(_kernel, (batch, toks, heads, npos, grou...  156 us

profile of v3, /device:TPU:112, one launch (start us, length us, event | category | flops | bytes accessed | tf_op | source)
XLA Modules:
  0.0 157.2 jit_solution(5848036916522904511)
XLA Ops:
  0.0 155.8 %mla_ring.1 = bf16[64,32,512]{2,1,0:T(8,128)(2,1)S(1)} custom-call(bf16[64,2,16,576]{3,2,1,0:T(8,128)(2,1)} %q_hbm.1, bf16[64,1024,576]{2,1,0:T(8,128)(2,1)} %bitcast.kv_hbm, s32[64]{0:T(128)} %len_ref.1), custom_call_target="tpu_custom_call" | custom-call | tf_op jit(solution)/shard_map/mla_ring/pallas_call | solution.py:323
  155.9 1.3 copy.5

commit v4 on v3

--- a/solution.py
+++ b/solution.py
@@ -19,12 +19,12 @@
 GO = 8
 KV_SLOTS = 4
 UNROLL = 2
-AHEAD = 2
+AHEAD = 3
 
 
 def _kernel(sizes, q_hbm, kv_hbm, len_ref, out_ref,
             qall, rope_in, kvb, o_all, prx, abuf, bbuf,
-            lse_all, plse, clse, alse, nlse, blse, wt,
+            lse_all, plse, clse, asnd, alse, bsnd, blse,
             load_sem, kv_sem, qs, qr, ds, dr, as_, ar, bs, br):
     batch, toks, heads, npos, group = sizes
     chips = group // CORES
@@ -101,8 +101,9 @@
     row_tok = (lax.broadcasted_iota(jnp.int32, (CORES * chips * rows, 1), 0) // heads) % toks
     key = lax.broadcasted_iota(jnp.int32, (1, npos), 1)
     pos = ((key // PAGE) * group + me) * PAGE + key % PAGE
-    lanes = chips * rows
-    eye = lax.broadcasted_iota(jnp.int32, (lanes, lanes), 0) == lax.broadcasted_iota(jnp.int32, (lanes, lanes), 1)
+    lanes = half * rows
+    shift = lax.broadcasted_iota(jnp.int32, (chips * rows, lanes), 1) - lax.broadcasted_iota(jnp.int32, (chips * rows, lanes), 0) % rows
+    lane_seq = lax.broadcasted_iota(jnp.int32, (chips, lanes), 1) // rows
 
     def scores(b):
         slot = lax.rem(b, KV_SLOTS)
@@ -125,9 +126,11 @@
         o = (o * (1.0 / l)).astype(jnp.bfloat16)
         o_all[:, :, b] = o.reshape(CORES, chips, rows, LATENT)
         lse = m * SCALE2 + jnp.log2(l)
+        place, in_half = b // half, b % half
         for kk in range(CORES):
-            col = lse[kk * lanes:(kk + 1) * lanes]
-            lse_all[kk, pl.ds(b, 1)] = jnp.sum(jnp.where(eye, col, 0.0), axis=0, keepdims=True)
+            col = lse[kk * chips * rows:(kk + 1) * chips * rows]
+            spread = jnp.where(shift == in_half * rows, col, 0.0).reshape(chips, rows, lanes)
+            lse_all[kk, place] = jnp.where(lane_seq == in_half, jnp.sum(spread, axis=1), lse_all[kk, place])
 
     def attend(b0):
         bs_ = [b0 + u for u in range(UNROLL)]
@@ -146,23 +149,36 @@
     def seqs(i, n=GO):
         return pl.ds(pl.multiple_of(i * n, n), n)
 
+    def halves(i):
+        return pl.ds(pl.multiple_of(2 * i, 2), 2)
+
+    def columns(rows_):
+        n = sum(r.shape[0] for r in rows_)
+        return jnp.transpose(jnp.concatenate(rows_ + [jnp.zeros((8 - n, lanes), jnp.float32)] if n < 8 else rows_, axis=0))
+
+    def merged(parts):
+        top = functools.reduce(jnp.maximum, parts)
+        total = top + jnp.log2(sum(jnp.exp2(x - top) for x in parts))
+        return total, [jnp.exp2(x - total) for x in parts]
+
     def d_send(i):
         return [rcopy(o_all.at[ok, :, seqs(i)], prx.at[:, seqs(i)], ds.at[0, i], dr.at[0, i], partner),
-                rcopy(lse_all.at[ok, seqs(i)], plse.at[seqs(i)], ds.at[1, i], dr.at[1, i], partner)]
+                rcopy(lse_all.at[ok, halves(i)], plse.at[halves(i)], ds.at[1, i], dr.at[1, i], partner)]
 
     def d_merge(i):
         for cp in d_send(i):
             cp.wait_recv()
-        a, b = lse_all[k, seqs(i)], plse[seqs(i)]
-        top = jnp.maximum(a, b)
-        both = top + jnp.log2(jnp.exp2(a - top) + jnp.exp2(b - top))
-        clse[seqs(i)] = both
-        wa, wb = jnp.transpose(jnp.exp2(a - both)), jnp.transpose(jnp.exp2(b - both))
+        w = []
+        for h in range(2):
+            total, (wa, wb) = merged([lse_all[k, 2 * i + h], plse[2 * i + h]])
+            clse[2 * i + h] = total
+            asnd[h, i] = clse[2 * i + h, pl.ds(cf, 1)]
+            w.append(columns([wa, wb]))
         for j in range(GO):
+            h, span = j // half, slice(j % half * rows, (j % half + 1) * rows)
             for cc in range(chips):
-                sl = slice(cc * rows, (cc + 1) * rows)
-                x = o_all[k, cc, i * GO + j].astype(jnp.float32) * wa[sl, j:j + 1]
-                y = prx[cc, i * GO + j].astype(jnp.float32) * wb[sl, j:j + 1]
+                x = o_all[k, cc, i * GO + j].astype(jnp.float32) * w[h][span, cc:cc + 1]
+                y = prx[cc, i * GO + j].astype(jnp.float32) * w[h][span, chips + cc:chips + cc + 1]
                 o_all[k, cc, i * GO + j] = (x + y).astype(jnp.bfloat16)
 
     def oreg(cc, i, part):
@@ -176,8 +192,8 @@
     def a_send(i):
         return [rcopy(oreg(cf, i, 0), abuf.at[0, pl.ds(i * half, half)], as_.at[0, i], ar.at[0, i], right),
                 rcopy(oreg(cf, i, 1), abuf.at[1, pl.ds(i * half, half)], as_.at[1, i], ar.at[1, i], left),
-                rcopy(clse.at[seqs(i)], alse.at[0, seqs(i)], as_.at[2, i], ar.at[2, i], right),
-                rcopy(clse.at[seqs(i)], alse.at[1, seqs(i)], as_.at[3, i], ar.at[3, i], left)]
+                rcopy(asnd.at[0, i], alse.at[0, i], as_.at[2, i], ar.at[2, i], right),
+                rcopy(asnd.at[1, i], alse.at[1, i], as_.at[3, i], ar.at[3, i], left)]
 
     def b_early(i):
         return [rcopy(oreg(cr, i, 1), breg(0, i, 1), bs.at[0, i], br.at[0, i], right),
@@ -186,47 +202,39 @@
     def b_late(i):
         return [rcopy(oreg(cr, i, 0), breg(0, i, 0), bs.at[2, i], br.at[2, i], right),
                 rcopy(oreg(cl, i, 1), breg(1, i, 1), bs.at[3, i], br.at[3, i], left),
-                rcopy(nlse.at[seqs(i)], blse.at[0, seqs(i)], bs.at[4, i], br.at[4, i], right),
-                rcopy(nlse.at[seqs(i)], blse.at[1, seqs(i)], bs.at[5, i], br.at[5, i], left)]
-
-    seq_id = lax.broadcasted_iota(jnp.int32, (GO, lanes), 0)
-    chip_id = lax.broadcasted_iota(jnp.int32, (GO, lanes), 1) // rows
-    from_left = (seq_id < half) & (chip_id == cr)
-    from_right = (seq_id >= half) & (chip_id == cl)
+                rcopy(bsnd.at[0, i], blse.at[0, i], bs.at[4, i], br.at[4, i], right),
+                rcopy(bsnd.at[1, i], blse.at[1, i], bs.at[5, i], br.at[5, i], left)]
 
     def a_merge(i):
         for cp in a_send(i):
             cp.wait_recv()
-        a = clse[seqs(i)]
-        b = jnp.where(from_left, alse[0, seqs(i)], jnp.where(from_right, alse[1, seqs(i)], a))
-        top = jnp.maximum(a, b)
-        both = top + jnp.log2(jnp.exp2(a - top) + jnp.exp2(b - top))
-        wt[0], wt[1] = jnp.transpose(jnp.exp2(a - both)), jnp.transpose(jnp.exp2(b - both))
-        nlse[seqs(i)] = jnp.where(from_left | from_right, both, a)
+        w, fresh = [], []
         for side, cc in ((0, cr), (1, cl)):
-            wa, wb = (wt[n, pl.ds(pl.multiple_of(cc * rows, rows), rows)] for n in range(2))
+            total, both = merged([clse[2 * i + side, pl.ds(cc, 1)], alse[side, i]])
+            fresh.append(total)
+            w += both
+        bsnd[0, i] = jnp.concatenate([fresh[0], clse[2 * i + 1, pl.ds(cr, 1)]], axis=0)
+        bsnd[1, i] = jnp.concatenate([clse[2 * i, pl.ds(cl, 1)], fresh[1]], axis=0)
+        w = columns(w)
+        for side, cc in ((0, cr), (1, cl)):
             for j in range(half):
-                lane = side * half + j
-                x = o_all[k, cc, i * GO + lane].astype(jnp.float32) * wa[:, lane:lane + 1]
-                y = abuf[side, i * half + j].astype(jnp.float32) * wb[:, lane:lane + 1]
-                o_all[k, cc, i * GO + lane] = (x + y).astype(jnp.bfloat16)
+                b, span = i * GO + side * half + j, slice(j * rows, (j + 1) * rows)
+                x = o_all[k, cc, b].astype(jnp.float32) * w[span, 2 * side:2 * side + 1]
+                y = abuf[side, i * half + j].astype(jnp.float32) * w[span, 2 * side + 1:2 * side + 2]
+                o_all[k, cc, b] = (x + y).astype(jnp.bfloat16)
         start(b_late(i))
 
     def final_merge(i):
         for cp in b_early(i) + b_late(i):
             cp.wait_recv()
         sent(b_late(i))
-        parts = [clse[seqs(i)], blse[0, seqs(i)], blse[1, seqs(i)]]
-        top = functools.reduce(jnp.maximum, parts)
-        total = top + jnp.log2(sum(jnp.exp2(x - top) for x in parts))
-        for n, x in enumerate(parts):
-            wt[n] = jnp.transpose(jnp.exp2(x - total))
-        w = [wt[n, pl.ds(pl.multiple_of(c * rows, rows), rows)] for n in range(3)]
+        own = jnp.concatenate([clse[2 * i + h, pl.ds(c, 1)] for h in range(2)], axis=0)
+        w = columns(merged([own, blse[0, i], blse[1, i]])[1])
         for j in range(GO):
-            b = i * GO + j
-            x = o_all[k, c, b].astype(jnp.float32) * w[0][:, j:j + 1]
-            x += bbuf[0, b].astype(jnp.float32) * w[1][:, j:j + 1]
-            x += bbuf[1, b].astype(jnp.float32) * w[2][:, j:j + 1]
+            b, h, span = i * GO + j, j // half, slice(j % half * rows, (j % half + 1) * rows)
+            x = o_all[k, c, b].astype(jnp.float32) * w[span, h:h + 1]
+            x += bbuf[0, b].astype(jnp.float32) * w[span, 2 + h:3 + h]
+            x += bbuf[1, b].astype(jnp.float32) * w[span, 4 + h:5 + h]
             out_ref[b] = x.astype(jnp.bfloat16)
 
     def sent(copies):
@@ -264,22 +272,9 @@
             for cp in q_far(j - 1):
                 cp.start()
 
-        @pl.when(j == n_q - 2)
-        def _():
-            start(a_send(0))
-
-        @pl.when(j == n_q - 1)
-        def _():
-            start(b_early(0))
-            ring_start(1, n_o // 2)
-
-        @pl.when(j == n_q)
-        def _():
-            ring_start(n_o // 2, n_o - 2)
-
-        @pl.when(j == n_q + 1)
-        def _():
-            ring_start(n_o - 2, n_o - 1)
+        for at, op in enumerate((lambda: start(a_send(0)), lambda: start(b_early(0)), lambda: ring_start(1, 2), lambda: ring_start(2, n_o // 2),
+                                 lambda: ring_start(n_o // 2, n_o - 2), lambda: ring_start(n_o - 2, n_o - 1))):
+            pl.when(j == n_q - 4 + at)(op)
 
         @pl.when(j >= 2)
         def _():
@@ -316,7 +311,7 @@
     def local_step(q_blk, kv_blk, len_blk):
         batch, toks, heads, width = q_blk.shape
         npos = kv_blk.shape[1] * kv_blk.shape[2] * kv_blk.shape[3]
-        rows, lanes = toks * heads, chips * toks * heads
+        rows, lanes = toks * heads, GO // 2 * toks * heads
         n_q, n_o = batch // GQ, batch // GO
         bf16, f32, dma = jnp.bfloat16, jnp.float32, pltpu.SemaphoreType.DMA
         any_space = pl.BlockSpec(memory_space=pl.ANY)
@@ -333,13 +328,13 @@
                 pltpu.VMEM((chips, batch, rows, LATENT), bf16),
                 pltpu.VMEM((2, batch // 2, rows, LATENT), bf16),
                 pltpu.VMEM((2, batch, rows, LATENT), bf16),
-                pltpu.VMEM((CORES, batch, lanes), f32),
-                pltpu.VMEM((batch, lanes), f32),
-                pltpu.VMEM((batch, lanes), f32),
-                pltpu.VMEM((2, batch, lanes), f32),
-                pltpu.VMEM((batch, lanes), f32),
-                pltpu.VMEM((2, batch, lanes), f32),
-                pltpu.VMEM((3, lanes, GO), f32),
+                pltpu.VMEM((CORES, 2 * n_o, chips, lanes), f32),
+                pltpu.VMEM((2 * n_o, chips, lanes), f32),
+                pltpu.VMEM((2 * n_o, chips, lanes), f32),
+                pltpu.VMEM((2, n_o, 1, lanes), f32),
+                pltpu.VMEM((2, n_o, 1, lanes), f32),
+                pltpu.VMEM((2, n_o, 2, lanes), f32),
+                pltpu.VMEM((2, n_o, 2, lanes), f32),
                 dma((2, toks + 1)), dma((KV_SLOTS,)),
                 dma((9, n_q)), dma((9, n_q)),
                 dma((2, n_o)), dma((2, n_o)),

time: 157 us -> 156 us (level)
  no operation moved by 1% of the time
where the time goes in v4:
time: 156 us
  Pallas kernels  155 us (99%)
    pallas_call x1, Pallas kernels, local_step(): pl.pallas_call(functools.partial(_kernel, (batch, toks, heads, npos, grou...  155 us

profile of v4, /device:TPU:112, one launch (start us, length us, event | category | flops | bytes accessed | tf_op | source)
XLA Modules:
  0.0 156.2 jit_solution(2101525469317956217)
XLA Ops:
  0.0 154.9 %mla_ring.1 = bf16[64,32,512]{2,1,0:T(8,128)(2,1)S(1)} custom-call(bf16[64,2,16,576]{3,2,1,0:T(8,128)(2,1)} %q_hbm.1, bf16[64,1024,576]{2,1,0:T(8,128)(2,1)} %bitcast.kv_hbm, s32[64]{0:T(128)} %len_ref.1), custom_call_target="tpu_custom_call" | custom-call | tf_op jit(solution)/shard_map/mla_ring/pallas_call | solution.py:318
  154.9 1.3 copy.5

commit v5 on v4

--- a/solution.py
+++ b/solution.py
@@ -22,10 +22,10 @@
 AHEAD = 3
 
 
-def _kernel(sizes, q_hbm, kv_hbm, len_ref, out_ref,
-            qall, rope_in, kvb, o_all, prx, abuf, bbuf,
+def _kernel(sizes, q_hbm, kv_hbm, len_hbm, out_ref,
+            len_ref, qall, rope_in, kvb, o_all, prx, abuf, bbuf,
             lse_all, plse, clse, asnd, alse, bsnd, blse,
-            load_sem, kv_sem, qs, qr, ds, dr, as_, ar, bs, br):
+            load_sem, len_sem, kv_sem, qs, qr, ds, dr, as_, ar, bs, br):
     batch, toks, heads, npos, group = sizes
     chips = group // CORES
     rows = toks * heads
@@ -68,6 +68,8 @@
     for n in range(2):
         lat, rope = q_loads(n)
         start([rope] + lat)
+    lengths = pltpu.make_async_copy(len_hbm, len_ref, len_sem)
+    lengths.start()
 
     def kv_copy(b):
         slot = lax.rem(b, KV_SLOTS)
@@ -200,10 +202,10 @@
                 rcopy(oreg(cl, i, 0), breg(1, i, 0), bs.at[1, i], br.at[1, i], left)]
 
     def b_late(i):
-        return [rcopy(oreg(cr, i, 0), breg(0, i, 0), bs.at[2, i], br.at[2, i], right),
-                rcopy(oreg(cl, i, 1), breg(1, i, 1), bs.at[3, i], br.at[3, i], left),
-                rcopy(bsnd.at[0, i], blse.at[0, i], bs.at[4, i], br.at[4, i], right),
-                rcopy(bsnd.at[1, i], blse.at[1, i], bs.at[5, i], br.at[5, i], left)]
+        return [rcopy(bsnd.at[0, i], blse.at[0, i], bs.at[4, i], br.at[4, i], right),
+                rcopy(bsnd.at[1, i], blse.at[1, i], bs.at[5, i], br.at[5, i], left),
+                rcopy(oreg(cr, i, 0), breg(0, i, 0), bs.at[2, i], br.at[2, i], right),
+                rcopy(oreg(cl, i, 1), breg(1, i, 1), bs.at[3, i], br.at[3, i], left)]
 
     def a_merge(i):
         for cp in a_send(i):
@@ -225,17 +227,20 @@
         start(b_late(i))
 
     def final_merge(i):
-        for cp in b_early(i) + b_late(i):
+        late = b_late(i)
+        for cp in b_early(i) + late[:2]:
             cp.wait_recv()
-        sent(b_late(i))
         own = jnp.concatenate([clse[2 * i + h, pl.ds(c, 1)] for h in range(2)], axis=0)
         w = columns(merged([own, blse[0, i], blse[1, i]])[1])
-        for j in range(GO):
-            b, h, span = i * GO + j, j // half, slice(j % half * rows, (j % half + 1) * rows)
-            x = o_all[k, c, b].astype(jnp.float32) * w[span, h:h + 1]
-            x += bbuf[0, b].astype(jnp.float32) * w[span, 2 + h:3 + h]
-            x += bbuf[1, b].astype(jnp.float32) * w[span, 4 + h:5 + h]
-            out_ref[b] = x.astype(jnp.bfloat16)
+        for h in range(2):
+            late[2 + h].wait_recv()
+            for j in range(half):
+                b, span = i * GO + h * half + j, slice(j * rows, (j + 1) * rows)
+                x = o_all[k, c, b].astype(jnp.float32) * w[span, h:h + 1]
+                x += bbuf[0, b].astype(jnp.float32) * w[span, 2 + h:3 + h]
+                x += bbuf[1, b].astype(jnp.float32) * w[span, 4 + h:5 + h]
+                out_ref[b] = x.astype(jnp.bfloat16)
+        sent(late)
 
     def sent(copies):
         for cp in copies:
@@ -251,6 +256,7 @@
     for b in range(KV_SLOTS):
         kv_copy(b).start()
     q_ready(1)
+    lengths.wait()
 
     def step(j, carry):
         @pl.when(j < n_q)
@@ -318,9 +324,10 @@
         out = pl.pallas_call(
             functools.partial(_kernel, (batch, toks, heads, npos, group)),
             out_shape=pltpu.VMEM((batch, rows, LATENT), bf16),
-            in_specs=[any_space, any_space, pl.BlockSpec(memory_space=pltpu.SMEM)],
+            in_specs=[any_space, any_space, any_space],
             out_specs=pl.BlockSpec(memory_space=pltpu.VMEM),
             scratch_shapes=[
+                pltpu.SMEM((batch,), jnp.int32),
                 pltpu.VMEM((CORES, chips, batch, heads, toks * width), bf16),
                 pltpu.VMEM((batch, toks, heads, ROPE), bf16),
                 pltpu.VMEM((KV_SLOTS, npos, width), bf16),
@@ -335,7 +342,7 @@
                 pltpu.VMEM((2, n_o, 1, lanes), f32),
                 pltpu.VMEM((2, n_o, 2, lanes), f32),
                 pltpu.VMEM((2, n_o, 2, lanes), f32),
-                dma((2, toks + 1)), dma((KV_SLOTS,)),
+                dma((2, toks + 1)), dma, dma((KV_SLOTS,)),
                 dma((9, n_q)), dma((9, n_q)),
                 dma((2, n_o)), dma((2, n_o)),
                 dma((4, n_o)), dma((4, n_o)),

time: 156 us -> 156 us (level)
  no operation moved by 1% of the time
where the time goes in v5:
time: 156 us; the launch traced here: 155 us
  Pallas kernels  154 us (99%)
    pallas_call x1, Pallas kernels, local_step(): pl.pallas_call(functools.partial(_kernel, (batch, toks, heads, npos, grou...  154 us

profile of v5, /device:TPU:112, one launch (start us, length us, event | category | flops | bytes accessed | tf_op | source)
XLA Modules:
  0.0 155.4 jit_solution(17925836370844829660)
XLA Ops:
  0.0 154.1 %mla_ring.1 = bf16[64,32,512]{2,1,0:T(8,128)(2,1)S(1)} custom-call(bf16[64,2,16,576]{3,2,1,0:T(8,128)(2,1)} %q_hbm.1, bf16[64,1024,576]{2,1,0:T(8,128)(2,1)} %bitcast.kv_hbm, s32[64]{0:T(128)} %len_hbm.1), custom_call_target="tpu_custom_call" | custom-call | tf_op jit(solution)/shard_map/mla_ring/pallas_call | solution.py:324
  154.1 1.3 copy.5

commit v6 on v5

--- a/solution.py
+++ b/solution.py
@@ -25,7 +25,7 @@
 def _kernel(sizes, q_hbm, kv_hbm, len_hbm, out_ref,
             len_ref, qall, rope_in, kvb, o_all, prx, abuf, bbuf,
             lse_all, plse, clse, asnd, alse, bsnd, blse,
-            load_sem, len_sem, kv_sem, qs, qr, ds, dr, as_, ar, bs, br):
+            turn, load_sem, len_sem, kv_sem, qs, qr, ds, dr, as_, ar, bs, br):
     batch, toks, heads, npos, group = sizes
     chips = group // CORES
     rows = toks * heads
@@ -210,6 +210,7 @@
     def a_merge(i):
         for cp in a_send(i):
             cp.wait_recv()
+        pl.when(i > 0)(lambda: start(b_late(i - 1)))
         w, fresh = [], []
         for side, cc in ((0, cr), (1, cl)):
             total, both = merged([clse[2 * i + side, pl.ds(cc, 1)], alse[side, i]])
@@ -224,7 +225,6 @@
                 x = o_all[k, cc, b].astype(jnp.float32) * w[span, 2 * side:2 * side + 1]
                 y = abuf[side, i * half + j].astype(jnp.float32) * w[span, 2 * side + 1:2 * side + 2]
                 o_all[k, cc, b] = (x + y).astype(jnp.bfloat16)
-        start(b_late(i))
 
     def final_merge(i):
         late = b_late(i)
@@ -251,8 +251,10 @@
 
     q_ready(0)
     pl.semaphore_wait(barrier, 3)
+    pl.when(k == CORES - 1)(lambda: pl.semaphore_wait(turn, 1))
     for j in range(AHEAD):
         start(q_own(j))
+    pl.when(k == 0)(lambda: pl.semaphore_signal(turn, inc=1, device_id={'dcp': partner}, device_id_type=pl.DeviceIdType.MESH))
     for b in range(KV_SLOTS):
         kv_copy(b).start()
     q_ready(1)
@@ -282,32 +284,37 @@
                                  lambda: ring_start(n_o // 2, n_o - 2), lambda: ring_start(n_o - 2, n_o - 1))):
             pl.when(j == n_q - 4 + at)(op)
 
+        @pl.when((j >= 4) & (j % 2 == 0))
+        def _():
+            start(d_send(j // 2 - 2))
+
         @pl.when(j >= 2)
         def _():
             s = j - 2
             for kind in (2, 5, 6, 7, 8):
                 q_arrival(kind, s).wait_recv()
             lax.fori_loop(0, GQ // UNROLL, lambda n, cc: (attend(s * GQ + n * UNROLL), cc)[1], 0)
-            i = s // 2
-
-            @pl.when(s % 2 == 1)
-            def _():
-                for cp in d_send(i):
-                    cp.start()
 
             @pl.when((s % 2 == 0) & (s > 0))
             def _():
-                d_merge(i - 1)
+                d_merge(s // 2 - 1)
 
         return carry
 
-    lax.fori_loop(0, n_q + 2, step, 0)
+    def each(lo, hi, op):
+        lax.fori_loop(lo, hi, lambda i, carry: (op(i), carry)[1], 0)
+
+    each(0, n_q + 2, lambda j: step(j, 0))
+    each(0, n_q // 2, lambda j: sent(q_own(j) + q_relay(j) + q_far(j)))
+    start(d_send(n_o - 1))
     d_merge(n_o - 1)
+    each(n_q // 2, n_q, lambda j: sent(q_own(j) + q_relay(j) + q_far(j)))
     ring_start(n_o - 1, n_o)
-    lax.fori_loop(0, n_q, lambda j, cc: (sent(q_own(j) + q_relay(j) + q_far(j)), cc)[1], 0)
-    lax.fori_loop(0, n_o, lambda i, cc: (a_merge(i), cc)[1], 0)
-    lax.fori_loop(0, n_o, lambda i, cc: (sent(d_send(i) + a_send(i) + b_early(i)), cc)[1], 0)
-    lax.fori_loop(0, n_o, lambda i, cc: (final_merge(i), cc)[1], 0)
+    each(0, n_o, a_merge)
+    each(0, n_o, lambda i: sent(d_send(i)))
+    start(b_late(n_o - 1))
+    each(0, n_o, lambda i: sent(a_send(i) + b_early(i)))
+    each(0, n_o, final_merge)
 
 
 def solution(mesh):
@@ -342,7 +349,7 @@
                 pltpu.VMEM((2, n_o, 1, lanes), f32),
                 pltpu.VMEM((2, n_o, 2, lanes), f32),
                 pltpu.VMEM((2, n_o, 2, lanes), f32),
-                dma((2, toks + 1)), dma, dma((KV_SLOTS,)),
+                pltpu.SemaphoreType.REGULAR, dma((2, toks + 1)), dma, dma((KV_SLOTS,)),
                 dma((9, n_q)), dma((9, n_q)),
                 dma((2, n_o)), dma((2, n_o)),
                 dma((4, n_o)), dma((4, n_o)),

time: 156 us -> 156 us (level)
  no operation moved by 1% of the time
where the time goes in v6:
time: 156 us
  Pallas kernels  155 us (99%)
    pallas_call x1, Pallas kernels, local_step(): pl.pallas_call(functools.partial(_kernel, (batch, toks, heads, npos, grou...  155 us

profile of v6, /device:TPU:112, one launch (start us, length us, event | category | flops | bytes accessed | tf_op | source)
XLA Modules:
  0.0 156.1 jit_solution(15715417834946585683)
XLA Ops:
  0.0 154.8 %mla_ring.1 = bf16[64,32,512]{2,1,0:T(8,128)(2,1)S(1)} custom-call(bf16[64,2,16,576]{3,2,1,0:T(8,128)(2,1)} %q_hbm.1, bf16[64,1024,576]{2,1,0:T(8,128)(2,1)} %bitcast.kv_hbm, s32[64]{0:T(128)} %len_hbm.1), custom_call_target="tpu_custom_call" | custom-call | tf_op jit(solution)/shard_map/mla_ring/pallas_call | solution.py:331
  154.8 1.3 copy.5

commit v7 on v6

--- a/solution.py
+++ b/solution.py
@@ -25,7 +25,7 @@
 def _kernel(sizes, q_hbm, kv_hbm, len_hbm, out_ref,
             len_ref, qall, rope_in, kvb, o_all, prx, abuf, bbuf,
             lse_all, plse, clse, asnd, alse, bsnd, blse,
-            turn, load_sem, len_sem, kv_sem, qs, qr, ds, dr, as_, ar, bs, br):
+            load_sem, len_sem, kv_sem, qs, qr, ds, dr, as_, ar, bs, br):
     batch, toks, heads, npos, group = sizes
     chips = group // CORES
     rows = toks * heads
@@ -65,11 +65,12 @@
         for cp in copies:
             cp.start()
 
-    for n in range(2):
+    def q_load(n):
         lat, rope = q_loads(n)
         start([rope] + lat)
+
+    q_load(0)
     lengths = pltpu.make_async_copy(len_hbm, len_ref, len_sem)
-    lengths.start()
 
     def kv_copy(b):
         slot = lax.rem(b, KV_SLOTS)
@@ -251,10 +252,10 @@
 
     q_ready(0)
     pl.semaphore_wait(barrier, 3)
-    pl.when(k == CORES - 1)(lambda: pl.semaphore_wait(turn, 1))
     for j in range(AHEAD):
         start(q_own(j))
-    pl.when(k == 0)(lambda: pl.semaphore_signal(turn, inc=1, device_id={'dcp': partner}, device_id_type=pl.DeviceIdType.MESH))
+    q_load(1)
+    lengths.start()
     for b in range(KV_SLOTS):
         kv_copy(b).start()
     q_ready(1)
@@ -349,7 +350,7 @@
                 pltpu.VMEM((2, n_o, 1, lanes), f32),
                 pltpu.VMEM((2, n_o, 2, lanes), f32),
                 pltpu.VMEM((2, n_o, 2, lanes), f32),
-                pltpu.SemaphoreType.REGULAR, dma((2, toks + 1)), dma, dma((KV_SLOTS,)),
+                dma((2, toks + 1)), dma, dma((KV_SLOTS,)),
                 dma((9, n_q)), dma((9, n_q)),
                 dma((2, n_o)), dma((2, n_o)),
                 dma((4, n_o)), dma((4, n_o)),

time: 156 us -> 156 us (level)
  no operation moved by 1% of the time
where the time goes in v7:
time: 156 us; the launch traced here: 155 us
  Pallas kernels  154 us (99%)
    pallas_call x1, Pallas kernels, local_step(): pl.pallas_call(functools.partial(_kernel, (batch, toks, heads, npos, grou...  154 us

profile of v7, /device:TPU:112, one launch (start us, length us, event | category | flops | bytes accessed | tf_op | source)
XLA Modules:
  0.0 155.4 jit_solution(953838502689078864)
XLA Ops:
  0.0 154.1 %mla_ring.1 = bf16[64,32,512]{2,1,0:T(8,128)(2,1)S(1)} custom-call(bf16[64,2,16,576]{3,2,1,0:T(8,128)(2,1)} %q_hbm.1, bf16[64,1024,576]{2,1,0:T(8,128)(2,1)} %bitcast.kv_hbm, s32[64]{0:T(128)} %len_hbm.1), custom_call_target="tpu_custom_call" | custom-call | tf_op jit(solution)/shard_map/mla_ring/pallas_call | solution.py:332
  154.1 1.3 copy.5

commit v8 on v7

--- a/solution.py
+++ b/solution.py
@@ -18,6 +18,7 @@
 GQ = 4
 GO = 8
 KV_SLOTS = 4
+OUT_COPIES = 4
 UNROLL = 2
 AHEAD = 3
 
@@ -316,6 +317,15 @@
     start(b_late(n_o - 1))
     each(0, n_o, lambda i: sent(a_send(i) + b_early(i)))
     each(0, n_o, final_merge)
+
+
+def _write_out(src, dst, sem):
+    n = src.shape[0] // OUT_COPIES
+    copies = [pltpu.make_async_copy(src.at[pl.ds(i * n, n)], dst.at[pl.ds(i * n, n)], sem.at[i]) for i in range(OUT_COPIES)]
+    for cp in copies:
+        cp.start()
+    for cp in copies:
+        cp.wait()
 
 
 def solution(mesh):
@@ -359,7 +369,14 @@
             compiler_params=pltpu.CompilerParams(collective_id=0, has_side_effects=True, vmem_limit_bytes=63_000_000),
             name='mla_ring',
         )(q_blk, kv_blk.reshape(batch, npos, width), len_blk)
-        return out.reshape(batch, toks, heads, LATENT)
+        return pl.pallas_call(
+            _write_out,
+            out_shape=jax.ShapeDtypeStruct((batch, rows, LATENT), bf16),
+            in_specs=[pl.BlockSpec(memory_space=pltpu.VMEM)],
+            out_specs=any_space,
+            scratch_shapes=[dma((OUT_COPIES,))],
+            name='write_out',
+        )(pltpu.with_memory_space_constraint(out, pltpu.VMEM)).reshape(batch, toks, heads, LATENT)
 
     return jax.shard_map(local_step, mesh=mesh, in_specs=(P('dp', None, 'dcp', None), P('dp', None, 'dcp', None, None), P('dp')),
                          out_specs=P('dp', None, 'dcp', None), check_vma=False)

time: 156 us -> 156 us (level)
  no operation moved by 1% of the time
where the time goes in v8:
time: 156 us; the launch traced here: 155 us
  Pallas kernels  155 us (99%)
    pallas_call x1, Pallas kernels, local_step(): pl.pallas_call(functools.partial(_kernel, (batch, toks, heads, npos, grou...  154 us

profile of v8, /device:TPU:112, one launch (start us, length us, event | category | flops | bytes accessed | tf_op | source)
XLA Modules:
  0.0 155.5 jit_solution(16472216818937500446)
XLA Ops:
  0.0 154.1 %mla_ring.1.src = bf16[64,32,512]{2,1,0:T(8,128)(2,1)S(1)} custom-call(bf16[64,2,16,576]{3,2,1,0:T(8,128)(2,1)} %q_hbm.1, bf16[64,1024,576]{2,1,0:T(8,128)(2,1)} %bitcast.kv_hbm, s32[64]{0:T(128)} %len_hbm.1), custom_call_target="tpu_custom_call" | custom-call | tf_op jit(solution)/shard_map/mla_ring/pallas_call | solution.py:342
  154.1 1.3 write_out.1

commit v9 on v7

--- a/solution.py
+++ b/solution.py
@@ -31,6 +31,7 @@
     rows = toks * heads
     half = GO // 2
     n_q, n_o = batch // GQ, batch // GO
+    lse_group = n_o // 2
     me = lax.axis_index('dcp')
     c, k = me // CORES, me % CORES
     ok = 1 - k
@@ -194,23 +195,35 @@
 
     def a_send(i):
         return [rcopy(oreg(cf, i, 0), abuf.at[0, pl.ds(i * half, half)], as_.at[0, i], ar.at[0, i], right),
-                rcopy(oreg(cf, i, 1), abuf.at[1, pl.ds(i * half, half)], as_.at[1, i], ar.at[1, i], left),
-                rcopy(asnd.at[0, i], alse.at[0, i], as_.at[2, i], ar.at[2, i], right),
-                rcopy(asnd.at[1, i], alse.at[1, i], as_.at[3, i], ar.at[3, i], left)]
+                rcopy(oreg(cf, i, 1), abuf.at[1, pl.ds(i * half, half)], as_.at[1, i], ar.at[1, i], left)]
+
+    def group_of(g):
+        return pl.ds(g * lse_group, lse_group)
+
+    def a_lse(g):
+        return [rcopy(asnd.at[0, group_of(g)], alse.at[0, group_of(g)], as_.at[2, g], ar.at[2, g], right),
+                rcopy(asnd.at[1, group_of(g)], alse.at[1, group_of(g)], as_.at[3, g], ar.at[3, g], left)]
+
+    def b_lse(g):
+        return [rcopy(bsnd.at[0, group_of(g)], blse.at[0, group_of(g)], bs.at[4, g], br.at[4, g], right),
+                rcopy(bsnd.at[1, group_of(g)], blse.at[1, group_of(g)], bs.at[5, g], br.at[5, g], left)]
+
+    def landed(copies):
+        for cp in copies:
+            cp.wait_recv()
 
     def b_early(i):
         return [rcopy(oreg(cr, i, 1), breg(0, i, 1), bs.at[0, i], br.at[0, i], right),
                 rcopy(oreg(cl, i, 0), breg(1, i, 0), bs.at[1, i], br.at[1, i], left)]
 
     def b_late(i):
-        return [rcopy(bsnd.at[0, i], blse.at[0, i], bs.at[4, i], br.at[4, i], right),
-                rcopy(bsnd.at[1, i], blse.at[1, i], bs.at[5, i], br.at[5, i], left),
-                rcopy(oreg(cr, i, 0), breg(0, i, 0), bs.at[2, i], br.at[2, i], right),
+        return [rcopy(oreg(cr, i, 0), breg(0, i, 0), bs.at[2, i], br.at[2, i], right),
                 rcopy(oreg(cl, i, 1), breg(1, i, 1), bs.at[3, i], br.at[3, i], left)]
 
     def a_merge(i):
-        for cp in a_send(i):
-            cp.wait_recv()
+        landed(a_send(i))
+        pl.when(i % lse_group == 0)(lambda: landed(a_lse(i // lse_group)))
+        pl.when(i == lse_group)(lambda: start(b_lse(0)))
         pl.when(i > 0)(lambda: start(b_late(i - 1)))
         w, fresh = [], []
         for side, cc in ((0, cr), (1, cl)):
@@ -229,12 +242,12 @@
 
     def final_merge(i):
         late = b_late(i)
-        for cp in b_early(i) + late[:2]:
-            cp.wait_recv()
+        landed(b_early(i))
+        pl.when(i % lse_group == 0)(lambda: landed(b_lse(i // lse_group)))
         own = jnp.concatenate([clse[2 * i + h, pl.ds(c, 1)] for h in range(2)], axis=0)
         w = columns(merged([own, blse[0, i], blse[1, i]])[1])
         for h in range(2):
-            late[2 + h].wait_recv()
+            late[h].wait_recv()
             for j in range(half):
                 b, span = i * GO + h * half + j, slice(j * rows, (j + 1) * rows)
                 x = o_all[k, c, b].astype(jnp.float32) * w[span, h:h + 1]
@@ -281,9 +294,9 @@
             for cp in q_far(j - 1):
                 cp.start()
 
-        for at, op in enumerate((lambda: start(a_send(0)), lambda: start(b_early(0)), lambda: ring_start(1, 2), lambda: ring_start(2, n_o // 2),
+        for at, op in enumerate((lambda: start(a_send(0)), lambda: start(b_early(0)), lambda: ring_start(1, 2), lambda: (ring_start(2, n_o // 2), start(a_lse(0))),
                                  lambda: ring_start(n_o // 2, n_o - 2), lambda: ring_start(n_o - 2, n_o - 1))):
-            pl.when(j == n_q - 4 + at)(op)
+            pl.when(j == n_q - 4 + at)(functools.partial(lambda f: (f(), None)[1], op))
 
         @pl.when((j >= 4) & (j % 2 == 0))
         def _():
@@ -311,11 +324,13 @@
     d_merge(n_o - 1)
     each(n_q // 2, n_q, lambda j: sent(q_own(j) + q_relay(j) + q_far(j)))
     ring_start(n_o - 1, n_o)
+    start(a_lse(1))
     each(0, n_o, a_merge)
     each(0, n_o, lambda i: sent(d_send(i)))
-    start(b_late(n_o - 1))
+    start(b_lse(1) + b_late(n_o - 1))
     each(0, n_o, lambda i: sent(a_send(i) + b_early(i)))
     each(0, n_o, final_merge)
+    each(0, 2, lambda g: sent(a_lse(g) + b_lse(g)))
 
 
 def solution(mesh):

time: 156 us -> 155 us (level)
  no operation moved by 1% of the time
where the time goes in v9:
time: 155 us
  Pallas kernels  154 us (99%)
    pallas_call x1, Pallas kernels, local_step(): pl.pallas_call(functools.partial(_kernel, (batch, toks, heads, npos, grou...  154 us

profile of v9, /device:TPU:112, one launch (start us, length us, event | category | flops | bytes accessed | tf_op | source)
XLA Modules:
  0.0 155.3 jit_solution(13771758492586832170)
XLA Ops:
  0.0 153.9 %mla_ring.1 = bf16[64,32,512]{2,1,0:T(8,128)(2,1)S(1)} custom-call(bf16[64,2,16,576]{3,2,1,0:T(8,128)(2,1)} %q_hbm.1, bf16[64,1024,576]{2,1,0:T(8,128)(2,1)} %bitcast.kv_hbm, s32[64]{0:T(128)} %len_hbm.1), custom_call_target="tpu_custom_call" | custom-call | tf_op jit(solution)/shard_map/mla_ring/pallas_call | solution.py:347
  153.9 1.3 copy.5

commit v10 on v9

--- a/solution.py
+++ b/solution.py
@@ -19,7 +19,7 @@
 GO = 8
 KV_SLOTS = 4
 UNROLL = 2
-AHEAD = 3
+AHEAD = 4
 
 
 def _kernel(sizes, q_hbm, kv_hbm, len_hbm, out_ref,

time: 155 us -> 155 us (level)
  no operation moved by 1% of the time
where the time goes in v10:
time: 155 us
  Pallas kernels  154 us (99%)
    pallas_call x1, Pallas kernels, local_step(): pl.pallas_call(functools.partial(_kernel, (batch, toks, heads, npos, grou...  154 us

profile of v10, /device:TPU:112, one launch (start us, length us, event | category | flops | bytes accessed | tf_op | source)
XLA Modules:
  0.0 155.3 jit_solution(12144291218358724185)
XLA Ops:
  0.0 154.0 %mla_ring.1 = bf16[64,32,512]{2,1,0:T(8,128)(2,1)S(1)} custom-call(bf16[64,2,16,576]{3,2,1,0:T(8,128)(2,1)} %q_hbm.1, bf16[64,1024,576]{2,1,0:T(8,128)(2,1)} %bitcast.kv_hbm, s32[64]{0:T(128)} %len_hbm.1), custom_call_target="tpu_custom_call" | custom-call | tf_op jit(solution)/shard_map/mla_ring/pallas_call | solution.py:347
  154.0 1.3 copy.5
